TPU v7x, 32 devices: a whole 2x2x4 slice. The times are simulated.
32 devices in a mesh: cx: 4 (over z), cy: 2 (over y), tp: 4 (over x, core).
Axes of the slice: x: 2, y: 2, z: 4, core: 2. Of those that a mesh axis runs over, the one named last changes fastest.
Arguments:
- neighbor_ids: int32 [16, 8, 128], P(('cx', 'cy'), 'tp'), may hold values from 0 to 1023
- decoder: bfloat16 [16, 64, 896], P(('cx', 'cy')), may hold values from -6 to 6
- table: bfloat16 [1024, 896], P(('cx', 'cy')), may hold values from -6 to 6
- attn_in: bfloat16 [6, 896, 896], P(None, ('cx', 'cy'), 'tp'), may hold values from -0.1875 to 0.1875
- attn_out: bfloat16 [2, 896, 896], P(None, 'tp', ('cx', 'cy')), may hold values from -0.1875 to 0.1875
- gains: float32 [3, 896], replicated, may hold values from 0.25 to 1.75
- w_up: bfloat16 [896, 3584], P(('cx', 'cy'), 'tp'), may hold values from -0.1875 to 0.1875
- w_down: bfloat16 [3584, 896], P('tp', ('cx', 'cy')), may hold values from -0.09375 to 0.09375
Outputs:
- encoded: bfloat16 [16, 8, 128, 896], P(('cx', 'cy'), 'tp')
All inputs are finite; a program needn't handle non-finite values.
Results may differ from a plain program's by a relative error of at most 0.013.
Values may be sent and summed in bfloat16 or wider, within the bound.
A program may use at most 128 MiB of HBM per device.

v0:
```python
import jax
import jax.numpy as jnp
from jax import lax
from jax.sharding import PartitionSpec as P

HD = 64


def layer_norm(values, gain):
    middle = jnp.mean(values, axis=-1, keepdims=True)
    centred = values - middle
    spread = jnp.mean(centred * centred, axis=-1, keepdims=True)
    return (centred * lax.rsqrt(spread + 1e-05) * gain).astype(jnp.bfloat16)


def project(hidden, matrix):
    return jnp.dot(hidden, matrix, preferred_element_type=jnp.float32).astype(jnp.bfloat16)


def attend(query, key_rows, value_rows):
    batch, q_len, width = query.shape
    k_len = key_rows.shape[1]
    heads = width // HD
    q_heads = query.reshape(batch, q_len, heads, HD)
    k_heads = key_rows.reshape(batch, k_len, heads, HD)
    v_heads = value_rows.reshape(batch, k_len, heads, HD)
    scores = jnp.einsum(
        "bqhd,bkhd->bhqk", q_heads, k_heads, preferred_element_type=jnp.float32
    ) * HD ** (-0.5)
    probs = jax.nn.softmax(scores, axis=-1).astype(jnp.bfloat16)
    mixed = jnp.einsum("bhqk,bkhd->bqhd", probs, v_heads, preferred_element_type=jnp.float32)
    return mixed.reshape(batch, q_len, width).astype(jnp.bfloat16)


def body(neighbor_ids, decoder, table, attn_in, attn_out, gains, w_up, w_down):
    full_table, in_w, out_w, up_w, down_w = (
        lax.all_gather(table, ("cx", "cy"), axis=0, tiled=True),
        lax.all_gather(attn_in, ("cx", "cy"), axis=1, tiled=True),
        lax.all_gather(attn_out, ("cx", "cy"), axis=2, tiled=True),
        lax.all_gather(w_up, ("cx", "cy"), axis=0, tiled=True),
        lax.all_gather(w_down, ("cx", "cy"), axis=1, tiled=True),
    )
    spans, nbrs, length = neighbor_ids.shape
    width = full_table.shape[1]
    dec_len = decoder.shape[1]
    total = spans * nbrs * length
    dec_rows = decoder.reshape(spans * dec_len, width)
    x_zero = jnp.take(full_table, neighbor_ids.reshape(-1), axis=0).astype(jnp.float32)
    h_one = layer_norm(x_zero, gains[0])
    in_full, out_full = (
        lax.all_gather(in_w, "tp", axis=2, tiled=True),
        lax.all_gather(out_w, "tp", axis=1, tiled=True),
    )
    query = project(h_one, in_full[0]).reshape(spans * nbrs, length, width)
    keys = project(h_one, in_full[1]).reshape(spans * nbrs, length, width)
    values = project(h_one, in_full[2]).reshape(spans * nbrs, length, width)
    self_out = attend(query, keys, values).reshape(total, width)
    x_one = x_zero + jnp.dot(self_out, out_full[0], preferred_element_type=jnp.float32)
    h_two = layer_norm(x_one, gains[1])
    cross_q = project(h_two, in_full[3]).reshape(spans, nbrs * length, width)
    cross_k = project(dec_rows, in_full[4]).reshape(spans, dec_len, width)
    cross_v = project(dec_rows, in_full[5]).reshape(spans, dec_len, width)
    cross = attend(cross_q, cross_k, cross_v).reshape(total, width)
    x_two = x_one + jnp.dot(cross, out_full[1], preferred_element_type=jnp.float32)
    h_three = layer_norm(x_two, gains[2])
    every = lax.all_gather(h_three, "tp", axis=0, tiled=True)
    upward = jnp.dot(every, up_w, preferred_element_type=jnp.float32)
    act = jax.nn.gelu(upward, approximate=True).astype(jnp.bfloat16)
    mixed = lax.psum_scatter(
        jnp.dot(act, down_w, preferred_element_type=jnp.float32).astype(jnp.bfloat16),
        "tp",
        scatter_dimension=0,
        tiled=True,
    ).astype(jnp.float32)
    return (x_two + mixed).astype(jnp.bfloat16).reshape(spans, nbrs, length, width)


def solution(mesh):
    in_specs = (
        P(("cx", "cy"), "tp", None),
        P(("cx", "cy"), None, None),
        P(("cx", "cy"), None),
        P(None, ("cx", "cy"), "tp"),
        P(None, "tp", ("cx", "cy")),
        P(),
        P(("cx", "cy"), "tp"),
        P("tp", ("cx", "cy")),
    )
    out_specs = P(("cx", "cy"), "tp", None, None)
    return jax.shard_map(body, mesh=mesh, in_specs=in_specs, out_specs=out_specs, check_vma=False)
```

profile of v0, /device:TPU:0, one launch (start us, length us, event | category | flops | bytes accessed | tf_op | source)
XLA Modules:
  0.0 414.2 jit_solution(9565664598188071752)
XLA Ops:
  9.3 69.2 %all-gather.10.cloned.1.call-done = bf16[6,896,224]{2,0,1:T(8,128)(2,1)} async-done(((bf16[6,112,224]{2,0,1:T(8,128)(2,1)}), bf16[6,896,224]{2,0,1:T(8,128)(2,1)}) %all-gather.10.cloned.1.call-update) | async-done | bytes 2408464 | tf_op jit(solution)/shard_map/all_gather | solution.py:38
  78.5 6.1 %copy.67 = bf16[6,896,224]{1,2,0:T(8,128)(2,1)} copy(bf16[6,896,224]{2,0,1:T(8,128)(2,1)} %all-gather.10.cloned.1.call-done) | data formatting | bytes 4816896 | tf_op jit(solution)/shard_map/all_gather | solution.py:38
  85.6 34.5 %all_gather.27 = bf16[2,224,896]{1,0,2:T(2,128)(2,1)S(1)} all-gather(bf16[2,224,112]{1,0,2:T(2,128)(2,1)S(1)} %copy.76), channel_id=1, replica_groups=mesh['cx'=4,'cy'=2,'tp'=4] {'cx','cy'}, dimensions={2}, use_global_device_ids=true | all-gather | bytes 903168 | tf_op jit(solution)/shard_map/all_gather | solution.py:39
  123.7 7.4 %all-gather.8.cloned.1.call-done = bf16[1024,896]{1,0:T(8,128)(2,1)} async-done(((bf16[128,896]{1,0:T(8,128)(2,1)}), bf16[1024,896]{1,0:T(8,128)(2,1)}) %all-gather.8.cloned.1.call-update) | async-done | bytes 1835024 | tf_op jit(solution)/shard_map/all_gather | solution.py:37
  131.1 4.3 %gather_fusion = bf16[512,896]{1,0:T(8,128)(2,1)S(1)} fusion(bf16[1024,896]{1,0:T(8,128)(2,1)} %all-gather.8.cloned.1.call-done, s32[1024]{0:T(1024)S(1)} %pad_clamp_fusion), kind=kCustom, calls=%fused_computation | custom fusion | bytes 1837056 | tf_op jit(solution)/shard_map/jit(_take)/gather | solution.py:48
  136.2 61.5 %all-gather.12.cloned.1.call-done = bf16[6,896,896]{1,2,0:T(8,128)(2,1)} async-done(((bf16[6,896,224]{1,2,0:T(8,128)(2,1)}), bf16[6,896,896]{1,2,0:T(8,128)(2,1)}) %all-gather.12.cloned.1.call-update) | async-done | bytes 9633808 | tf_op jit(solution)/shard_map/all_gather | solution.py:51
  197.7 3.8 fusion.46
  201.5 2.9 reshape.106
  204.4 3.9 fusion.47
  208.3 4.0 reshape.107
  212.3 3.0 fusion.29
  215.3 2.7 fusion.82
  218.0 3.8 fusion.45
  221.7 3.1 reshape.105
  224.8 2.8 fusion.52
  228.4 2.8 fusion.83
  232.4 2.8 fusion.48
  239.0 2.7 fusion.56
  249.3 2.8 fusion.85
  253.7 21.0 %all-gather.18.cloned.1.call-done = bf16[896,896]{1,0:T(8,128)(2,1)} async-done(((bf16[112,896]{1,0:T(8,128)(2,1)}), bf16[896,896]{1,0:T(8,128)(2,1)}) %all-gather.18.cloned.1.call-update) | async-done | bytes 1605648 | tf_op jit(solution)/shard_map/all_gather | solution.py:40
  274.7 45.0 %all-gather.20.cloned.1.call-done = bf16[896,896]{0,1:T(8,128)(2,1)} async-done(((bf16[896,112]{0,1:T(8,128)(2,1)}), bf16[896,896]{0,1:T(8,128)(2,1)}) %all-gather.20.cloned.1.call-update) | async-done | bytes 1605648 | tf_op jit(solution)/shard_map/all_gather | solution.py:41
  319.7 31.4 %all-gather.16.cloned.1.call-done = bf16[2048,896]{1,0:T(8,128)(2,1)} async-done(((bf16[512,896]{1,0:T(8,128)(2,1)}), bf16[2048,896]{1,0:T(8,128)(2,1)}) %all-gather.16.cloned.1.call-update) | async-done | bytes 3670032 | tf_op jit(solution)/shard_map/all_gather | solution.py:66
  351.1 12.6 %fusion.16 = bf16[2048,896]{1,0:T(8,128)(2,1)} fusion(bf16[896,896]{0,1:T(8,128)(2,1)} %all-gather.20.cloned.1.call-done, bf16[2048,896]{1,0:T(8,128)(2,1)} %all-gather.16.cloned.1.call-done, bf16[896,896]{1,0:T(8,128)(2,1)} %all-gather.18.cloned.1.call-done), kind=kOutput, calls=%fused_computation.19 | convolution fusion | flops 6595018752 | bytes 10551296 | tf_op jit(solution)/shard_map/dot_general | solution.py:70
  363.7 41.4 %reduce-scatter.2.cloned.1.call-done = bf16[512,896]{1,0:T(8,128)(2,1)} async-done(((bf16[2048,896]{1,0:T(8,128)(2,1)}), bf16[512,896]{1,0:T(8,128)(2,1)}) %reduce-scatter.2.cloned.1.call-update) | async-done | bytes 917520 | tf_op jit(solution)/shard_map/reduce_scatter | solution.py:69
  (62 shorter events, 25.3 us)
Async XLA Ops:
  6.5 230.0 %copy-start = (bf16[2,64,896]{2,1,0:T(8,128)(2,1)S(1)}, bf16[2,64,896]{2,1,0:T(8,128)(2,1)}, u32[]{:S(2)}) copy-start(bf16[2,64,896]{2,1,0:T(8,128)(2,1)} %param.9) | copy-start | bytes 688132
  6.5 71.9 %all-gather.10.cloned.1.call-start = ((), (), s32[]{:S(2)}) async-start(), calls=%async_computation.2 | async-start | bytes 4128768 | tf_op jit(solution)/shard_map/all_gather | solution.py:38
  8.5 122.6 %all-gather.8.cloned.1.call-start = ((), (), s32[]{:S(2)}) async-start(), calls=%async_computation.1 | async-start | bytes 2064384 | tf_op jit(solution)/shard_map/all_gather | solution.py:37
  9.2 188.5 %all-gather.12.cloned.1.call-start = ((), (), s32[]{:S(2)}) async-start(), calls=%async_computation.3 | async-start | bytes 12042240 | tf_op jit(solution)/shard_map/all_gather | solution.py:51
  84.6 0.9 copy-start.5
  84.6 143.8 %all-gather.14.cloned.1.call-start = ((), (), s32[]{:S(2)}) async-start(), calls=%async_computation.4 | async-start | bytes 4014080 | tf_op jit(solution)/shard_map/all_gather | solution.py:52
  85.6 38.0 %copy-start.6 = (s32[2,2,128]{2,1,0:T(2,128)S(1)}, s32[2,2,128]{2,1,0:T(2,128)}, u32[]{:S(2)}) copy-start(s32[2,2,128]{2,1,0:T(2,128)} %param.8) | copy-start | bytes 6148
  85.6 38.0 %copy-start.7 = (f32[3,896]{1,0:T(4,128)S(1)}, f32[3,896]{1,0:T(4,128)}, u32[]{:S(2)}) copy-start(f32[3,896]{1,0:T(4,128)} %param.13) | copy-start | bytes 32260
  122.4 152.3 %all-gather.18.cloned.1.call-start = ((), (), s32[]{:S(2)}) async-start(), calls=%async_computation.6 | async-start | bytes 1806336 | tf_op jit(solution)/shard_map/all_gather | solution.py:40
  122.9 196.7 %all-gather.20.cloned.1.call-start = ((), (), s32[]{:S(2)}) async-start(), calls=%async_computation.7 | async-start | bytes 1806336 | tf_op jit(solution)/shard_map/all_gather | solution.py:41
  123.5 227.6 %all-gather.16.cloned.1.call-start = ((), (), s32[]{:S(2)}) async-start(), calls=%async_computation.5 | async-start | bytes 4587520 | tf_op jit(solution)/shard_map/all_gather | solution.py:66
  231.2 1.2 copy-start.2
  243.8 1.3 copy-start.4
  247.8 1.5 copy-start.3
  253.7 151.4 %reduce-scatter.2.cloned.1.call-start = ((), (), s32[]{:S(2)}) async-start(), calls=%async_computation.8 | async-start | bytes 4587520 | tf_op jit(solution)/shard_map/reduce_scatter | solution.py:69
  363.7 43.6 %copy-start.1 = (bf16[2,64,896]{2,1,0:T(8,128)(2,1)S(1)}, bf16[2,64,896]{2,1,0:T(8,128)(2,1)}, u32[]{:S(2)}) copy-start(bf16[2,64,896]{2,1,0:T(8,128)(2,1)} %param.9) | copy-start | bytes 688132
Sparse Core Ops, SparseCore 0:
  9.5 68.9 all-gather.9
  80.7 50.3 all-gather.7
  132.6 65.0 all-gather.11
  199.1 28.8 all-gather.13
  230.1 44.5 all-gather.17
  276.7 42.9 all-gather.19
  321.2 29.8 all-gather.15
  363.8 41.2 reduce-scatter.1
where the time goes:
time: 415 us; the launch traced here: 414 us
  waiting for transfers between devices  279 us (67%)
  matrix products  45.8 us (11%)
  blocking collectives  34.5 us (8%)
  local copies, waits for them, and re-layouts  32.9 us (8%)
  between operations  13.7 us (3%)
  other arithmetic  8.18 us (2%)
    all_gather x1, waiting for transfers between devices, body(): lax.all_gather(attn_in, ('cx', 'cy'), axis=1, tiled=True)  69.2 us
    all_gather x1, waiting for transfers between devices, body(): lax.all_gather(in_w, 'tp', axis=2, tiled=True)  61.5 us
    all_gather x1, waiting for transfers between devices, body(): lax.all_gather(w_down, ('cx', 'cy'), axis=1, tiled=True)  45 us
    reduce_scatter x1, waiting for transfers between devices, body(): lax.psum_scatter(jnp.dot(act, down_w, preferred_element_type=jnp.float32)...  41.4 us
    all_gather x1, blocking collectives, body(): lax.all_gather(attn_out, ('cx', 'cy'), axis=2, tiled=True)  34.5 us
    all_gather x1, waiting for transfers between devices, body(): every = lax.all_gather(h_three, 'tp', axis=0, tiled=True)  31.4 us
    all_gather x1, waiting for transfers between devices, body(): lax.all_gather(w_up, ('cx', 'cy'), axis=0, tiled=True)  21 us
    dot_general x6, matrix products, project(): jnp.dot(hidden, matrix, preferred_element_type=jnp.float32)  18.9 us
  transfers between devices with their start and end apart: 8, of which 7 were waited for; matrix products, arithmetic and copies ran while one was open for 16% of the time, Pallas kernels for 0%

commit v1 on v0

--- a/solution.py
+++ b/solution.py
@@ -33,10 +33,12 @@
 
 
 def body(neighbor_ids, decoder, table, attn_in, attn_out, gains, w_up, w_down):
-    full_table, in_w, out_w, up_w, down_w = (
+    rows, cols = attn_in.shape[1:]
+    packed = jnp.concatenate([attn_in, attn_out.transpose(0, 2, 1)], axis=0)
+    packed = packed.transpose(1, 0, 2).reshape(rows, -1)
+    full_table, every_w, up_w, down_w = (
         lax.all_gather(table, ("cx", "cy"), axis=0, tiled=True),
-        lax.all_gather(attn_in, ("cx", "cy"), axis=1, tiled=True),
-        lax.all_gather(attn_out, ("cx", "cy"), axis=2, tiled=True),
+        lax.all_gather(packed, ("cx", "cy", "tp"), axis=0, tiled=True),
         lax.all_gather(w_up, ("cx", "cy"), axis=0, tiled=True),
         lax.all_gather(w_down, ("cx", "cy"), axis=1, tiled=True),
     )
@@ -47,21 +49,21 @@
     dec_rows = decoder.reshape(spans * dec_len, width)
     x_zero = jnp.take(full_table, neighbor_ids.reshape(-1), axis=0).astype(jnp.float32)
     h_one = layer_norm(x_zero, gains[0])
-    in_full, out_full = (
-        lax.all_gather(in_w, "tp", axis=2, tiled=True),
-        lax.all_gather(out_w, "tp", axis=1, tiled=True),
-    )
+    shards = lax.axis_size("tp")
+    whole = every_w.reshape(-1, shards, rows, attn_in.shape[0] + attn_out.shape[0], cols)
+    whole = whole.transpose(3, 0, 2, 1, 4).reshape(-1, width, width)
+    in_full, out_full = whole[: attn_in.shape[0]], whole[attn_in.shape[0] :]
     query = project(h_one, in_full[0]).reshape(spans * nbrs, length, width)
     keys = project(h_one, in_full[1]).reshape(spans * nbrs, length, width)
     values = project(h_one, in_full[2]).reshape(spans * nbrs, length, width)
     self_out = attend(query, keys, values).reshape(total, width)
-    x_one = x_zero + jnp.dot(self_out, out_full[0], preferred_element_type=jnp.float32)
+    x_one = x_zero + jnp.dot(self_out, out_full[0].T, preferred_element_type=jnp.float32)
     h_two = layer_norm(x_one, gains[1])
     cross_q = project(h_two, in_full[3]).reshape(spans, nbrs * length, width)
     cross_k = project(dec_rows, in_full[4]).reshape(spans, dec_len, width)
     cross_v = project(dec_rows, in_full[5]).reshape(spans, dec_len, width)
     cross = attend(cross_q, cross_k, cross_v).reshape(total, width)
-    x_two = x_one + jnp.dot(cross, out_full[1], preferred_element_type=jnp.float32)
+    x_two = x_one + jnp.dot(cross, out_full[1].T, preferred_element_type=jnp.float32)
     h_three = layer_norm(x_two, gains[2])
     every = lax.all_gather(h_three, "tp", axis=0, tiled=True)
     upward = jnp.dot(every, up_w, preferred_element_type=jnp.float32)

time: 415 us -> 390 us (0.940)
  local copies, waits for them, and re-layouts: 32.9 us -> 107 us
  waiting for transfers between devices: 279 us -> 213 us
  blocking collectives: 34.5 us -> 0 us
    reshape x0 -> x3, local copies, waits for them, and re-layouts: none -> 47.4 us  [the longest x2 46.2 us: body(): every_w.reshape(-1, shards, rows, attn_in.shape[0] + attn_out.shape[0], c...]
    all_gather x1, waiting for transfers between devices: 45 us -> 0.02 us  [body(): lax.all_gather(w_down, ('cx', 'cy'), axis=1, tiled=True)]
    all_gather x1, waiting for transfers between devices: 7.41 us -> 46.4 us  [body(): lax.all_gather(table, ('cx', 'cy'), axis=0, tiled=True)]
    all_gather x3 -> x1, waiting for transfers between devices: 131 us -> 92.9 us  [body(): lax.all_gather(packed, ('cx', 'cy', 'tp'), axis=0, tiled=True)]
    all_gather x1 -> x0, blocking collectives: 34.5 us -> none  [body(): lax.all_gather(attn_out, ('cx', 'cy'), axis=2, tiled=True)]
    squeeze x0 -> x8, local copies, waits for them, and re-layouts: none -> 26.2 us  [the longest x1 4.33 us: body(): cross_v = project(dec_rows, in_full[5]).reshape(spans, dec_len, width)]
    all_gather x1, waiting for transfers between devices: 21 us -> 0.02 us  [body(): lax.all_gather(w_up, ('cx', 'cy'), axis=0, tiled=True)]
    slice x0 -> x1, local copies, waits for them, and re-layouts: none -> 10.3 us  [body(): out_full[1]]
  transfers between devices with their start and end apart: 8 -> 6, of which waited for: 7 -> 4; matrix products, arithmetic and copies ran while one was open for 16% -> 37% of each run, Pallas kernels for 0% -> 0%
where the time goes in v1:
time: 390 us; the launch traced here: 388 us
  waiting for transfers between devices  213 us (55%)
  local copies, waits for them, and re-layouts  107 us (27%)
  matrix products  44.3 us (11%)
  between operations  13.8 us (4%)
  other arithmetic  9.24 us (2%)
    all_gather x1, waiting for transfers between devices, body(): lax.all_gather(packed, ('cx', 'cy', 'tp'), axis=0, tiled=True)  92.9 us
    all_gather x1, waiting for transfers between devices, body(): lax.all_gather(table, ('cx', 'cy'), axis=0, tiled=True)  46.4 us
    reshape x2, local copies, waits for them, and re-layouts, body(): every_w.reshape(-1, shards, rows, attn_in.shape[0] + attn_out.shape[0], c...  46.2 us
    reduce_scatter x1, waiting for transfers between devices, body(): lax.psum_scatter(jnp.dot(act, down_w, preferred_element_type=jnp.float32)...  41.4 us
    all_gather x1, waiting for transfers between devices, body(): every = lax.all_gather(h_three, 'tp', axis=0, tiled=True)  30.3 us
    dot_general x6, matrix products, project(): jnp.dot(hidden, matrix, preferred_element_type=jnp.float32)  16.6 us
    dot_general x1, matrix products, body(): jnp.dot(act, down_w, preferred_element_type=jnp.float32)  12.5 us
    slice x1, local copies, waits for them, and re-layouts, body(): out_full[1]  10.3 us
  transfers between devices with their start and end apart: 6, of which 4 were waited for; matrix products, arithmetic and copies ran while one was open for 37% of the time, Pallas kernels for 0%

profile of v1, /device:TPU:0, one launch (start us, length us, event | category | flops | bytes accessed | tf_op | source)
XLA Modules:
  0.0 387.7 jit_solution(5940456811100940443)
XLA Ops:
  12.3 46.4 %all-gather.6.cloned.1.call-done = bf16[1024,896]{1,0:T(8,128)(2,1)} async-done(((bf16[128,896]{1,0:T(8,128)(2,1)}), bf16[1024,896]{1,0:T(8,128)(2,1)}) %all-gather.6.cloned.1.call-update) | async-done | bytes 1835024 | tf_op jit(solution)/shard_map/all_gather | solution.py:40
  58.7 4.3 %gather_fusion = bf16[512,896]{1,0:T(8,128)(2,1)S(1)} fusion(bf16[1024,896]{1,0:T(8,128)(2,1)} %all-gather.6.cloned.1.call-done, s32[1024]{0:T(1024)S(1)} %pad_clamp_fusion), kind=kCustom, calls=%fused_computation | custom fusion | bytes 1837056 | tf_op jit(solution)/shard_map/jit(_take)/gather | solution.py:50
  63.8 92.9 %all-gather.8.cloned.1.call-done = bf16[3584,1792]{1,0:T(8,128)(2,1)} async-done(((bf16[112,1792]{1,0:T(8,128)(2,1)}), bf16[3584,1792]{1,0:T(8,128)(2,1)}) %all-gather.8.cloned.1.call-update) | async-done | bytes 12845072 | tf_op jit(solution)/shard_map/all_gather | solution.py:41
  156.6 28.8 %reshape.121 = bf16[8,4,112,8,224]{4,3,2,1,0:T(8,128)(2,1)} reshape(bf16[3584,1792]{1,0:T(8,128)(2,1)} %all-gather.8.cloned.1.call-done) | data formatting | bytes 25690112 | tf_op jit(solution)/shard_map/reshape | solution.py:53
  185.5 17.4 %copy.19 = bf16[8,4,112,8,224]{2,0,4,1,3:T(8,128)(2,1)} copy(bf16[8,4,112,8,224]{4,3,2,1,0:T(8,128)(2,1)} %reshape.121) | data formatting | bytes 25690112 | tf_op jit(solution)/shard_map/reshape | solution.py:53
  202.8 10.3 %fusion.69 = (bf16[1,8,112,4,224]{2,1,4,3,0:T(8,128)(2,1)}, bf16[1,8,112,4,224]{2,1,4,3,0:T(8,128)(2,1)}, bf16[1,8,112,4,224]{2,1,4,3,0:T(8,128)(2,1)}, bf16[1,8...) fusion(bf16[8,8,112,4,224]{2,1,4,3,0:T(8,128)(2,1)} %bitcast.83), kind=kLoop, calls=%fused_computation.91 | loop fusion | bytes 25690112 | tf_op jit(solution)/shard_map/slice | solution.py:66
  213.1 4.1 %squeeze.27 = bf16[896,896]{0,1:T(8,128)(2,1)} reshape(bf16[1,8,112,4,224]{2,1,4,3,0:T(8,128)(2,1)} %get-tuple-element.12) | data formatting | bytes 3211264 | tf_op jit(solution)/shard_map/squeeze | solution.py:60
  219.6 3.8 convolution_convert_fusion.1
  223.4 2.9 reshape.134
  226.3 4.1 %squeeze.25 = bf16[896,896]{0,1:T(8,128)(2,1)} reshape(bf16[1,8,112,4,224]{2,1,4,3,0:T(8,128)(2,1)} %get-tuple-element.14) | data formatting | bytes 3211264 | tf_op jit(solution)/shard_map/squeeze | solution.py:56
  230.4 3.8 convolution_convert_fusion.2
  234.2 4.0 %reshape.133 = bf16[4,128,14,64]{3,2,1,0:T(8,128)(2,1)} reshape(bf16[512,896]{1,0:T(8,128)(2,1)} %convolution_convert_fusion.2) | data formatting | bytes 1835008 | tf_op jit(solution)/shard_map/reshape;reshape | solution.py:24
  238.2 3.0 fusion.29
  241.2 2.7 fusion.70
  246.3 3.8 convolution_convert_fusion.3
  250.1 2.9 reshape.132
  253.0 2.7 fusion.39
  259.8 3.1 fusion.71
  267.7 4.1 %squeeze.30 = bf16[896,896]{0,1:T(8,128)(2,1)} reshape(bf16[1,8,112,4,224]{2,1,4,3,0:T(8,128)(2,1)} %get-tuple-element.9) | data formatting | bytes 3211264 | tf_op jit(solution)/shard_map/squeeze | solution.py:63
  274.0 4.3 %squeeze.28 = bf16[896,896]{0,1:T(8,128)(2,1)} reshape(bf16[1,8,112,4,224]{2,1,4,3,0:T(8,128)(2,1)} %get-tuple-element.11) | data formatting | bytes 3211264 | tf_op jit(solution)/shard_map/squeeze | solution.py:64
  289.3 3.3 fusion.73
  294.3 30.3 %all-gather.10.cloned.1.call-done = bf16[2048,896]{1,0:T(8,128)(2,1)} async-done(((bf16[512,896]{1,0:T(8,128)(2,1)}), bf16[2048,896]{1,0:T(8,128)(2,1)}) %all-gather.10.cloned.1.call-update) | async-done | bytes 3670032 | tf_op jit(solution)/shard_map/all_gather | solution.py:68
  324.6 12.5 %fusion.16 = bf16[2048,896]{1,0:T(8,128)(2,1)} fusion(bf16[896,896]{0,1:T(8,128)(2,1)} %all-gather.14.cloned.1.call-done, bf16[2048,896]{1,0:T(8,128)(2,1)} %all-gather.10.cloned.1.call-done, bf16[896,896]{1,0:T(8,128)(2,1)} %all-gather.12.cloned.1.call-done), kind=kOutput, calls=%fused_computation.19 | convolution fusion | flops 6595018752 | bytes 10551296 | tf_op jit(solution)/shard_map/dot_general | solution.py:72
  337.2 41.4 %reduce-scatter.2.cloned.1.call-done = bf16[512,896]{1,0:T(8,128)(2,1)} async-done(((bf16[2048,896]{1,0:T(8,128)(2,1)}), bf16[512,896]{1,0:T(8,128)(2,1)}) %reduce-scatter.2.cloned.1.call-update) | async-done | bytes 917520 | tf_op jit(solution)/shard_map/reduce_scatter | solution.py:71
  (68 shorter events, 37.1 us)
Async XLA Ops:
  6.5 265.3 %copy-start = (bf16[2,64,896]{2,1,0:T(8,128)(2,1)S(1)}, bf16[2,64,896]{2,1,0:T(8,128)(2,1)}, u32[]{:S(2)}) copy-start(bf16[2,64,896]{2,1,0:T(8,128)(2,1)} %param.9) | copy-start | bytes 688132
  6.5 52.1 %all-gather.6.cloned.1.call-start = ((), (), s32[]{:S(2)}) async-start(), calls=%async_computation.1 | async-start | bytes 2064384 | tf_op jit(solution)/shard_map/all_gather | solution.py:40
  7.3 149.4 %all-gather.8.cloned.1.call-start = ((), (), s32[]{:S(2)}) async-start(), calls=%async_computation.2 | async-start | bytes 13246464 | tf_op jit(solution)/shard_map/all_gather | solution.py:41
  7.3 4.9 %copy-start.8 = (f32[3,896]{1,0:T(4,128)S(1)}, f32[3,896]{1,0:T(4,128)}, u32[]{:S(2)}) copy-start(f32[3,896]{1,0:T(4,128)} %param.13) | copy-start | bytes 32260
  7.3 4.9 %copy-start.7 = (s32[2,2,128]{2,1,0:T(2,128)S(1)}, s32[2,2,128]{2,1,0:T(2,128)}, u32[]{:S(2)}) copy-start(s32[2,2,128]{2,1,0:T(2,128)} %param.8) | copy-start | bytes 6148
  10.8 283.5 %all-gather.14.cloned.1.call-start = ((), (), s32[]{:S(2)}) async-start(), calls=%async_computation.5 | async-start | bytes 1806336 | tf_op jit(solution)/shard_map/all_gather | solution.py:43
  11.6 282.7 %all-gather.12.cloned.1.call-start = ((), (), s32[]{:S(2)}) async-start(), calls=%async_computation.4 | async-start | bytes 1806336 | tf_op jit(solution)/shard_map/all_gather | solution.py:42
  12.1 312.5 %all-gather.10.cloned.1.call-start = ((), (), s32[]{:S(2)}) async-start(), calls=%async_computation.3 | async-start | bytes 4587520 | tf_op jit(solution)/shard_map/all_gather | solution.py:68
  241.2 2.7 copy-start.3
  255.7 1.7 copy-start.2
  262.9 1.3 copy-start.4
  262.9 2.1 copy-start.6
  281.4 1.2 copy-start.5
  285.4 1.5 copy-start.1
  294.2 84.4 %reduce-scatter.2.cloned.1.call-start = ((), (), s32[]{:S(2)}) async-start(), calls=%async_computation.6 | async-start | bytes 4587520 | tf_op jit(solution)/shard_map/reduce_scatter | solution.py:71
Sparse Core Ops, SparseCore 0:
  9.5 49.0 all-gather.5
  61.5 95.1 all-gather.7
  158.8 43.1 all-gather.13
  204.0 42.9 all-gather.11
  294.3 30.2 all-gather.9
  337.3 41.2 reduce-scatter.1
